TPU v7x, 8 devices: a whole 2x2x1 slice. The times are simulated.
8 devices in a mesh: rep: 2 (over z, y), dp: 4 (over x, core).
Axes of the slice: x: 2, y: 2, z: 1, core: 2. Of those that a mesh axis runs over, the one named last changes fastest.
Arguments:
- hidden: bfloat16 [512, 7168], P(('rep', 'dp')), parts along dimension 0
- ckv_cache: bfloat16 [512, 512, 512], P(('rep', 'dp')), parts along dimension 0
- kpe_cache: bfloat16 [512, 512, 64], P(('rep', 'dp')), parts along dimension 0
- cache_len: int32 [512], P(('rep', 'dp')), parts along dimension 0
- rope_cos: float32 [512, 32], P(('rep', 'dp')), parts along dimension 0
- rope_sin: float32 [512, 32], P(('rep', 'dp')), parts along dimension 0
- norm_attn: float32 [7168], replicated
- w_dq: bfloat16 [7168, 1536], replicated
- norm_q: float32 [1536], replicated
- w_uq: bfloat16 [1536, 64, 192], replicated
- w_dkv: bfloat16 [7168, 576], replicated
- norm_kv: float32 [512], replicated
- w_uk: bfloat16 [512, 64, 128], replicated
- w_uv: bfloat16 [512, 64, 128], replicated
- w_out: bfloat16 [64, 128, 7168], replicated
- norm_mlp: float32 [7168], replicated
- w_gate: bfloat16 [7168, 18432], P(None, 'dp')
- w_up: bfloat16 [7168, 18432], P(None, 'dp')
- w_down: bfloat16 [18432, 7168], P('dp')
Outputs:
- output 1: bfloat16 [512, 7168], P(('rep', 'dp')), parts along dimension 0
- output 2: bfloat16 [512, 512], P(('rep', 'dp')), parts along dimension 0
- output 3: bfloat16 [512, 64], P(('rep', 'dp')), parts along dimension 0
There are 2 independent parts. A program takes and returns all parts, laid end to end along the dimension named above; an argument that names none is the same for every part.
All inputs are finite; a program needn't handle non-finite values.
Results may differ from a plain program's by a relative error of at most 0.0108563.
Values are sent between devices in bfloat16 or wider.
A program may use at most 1.75 GiB of HBM per device.

v0:
```python
import functools
import math
import jax
import jax.numpy as jnp
from jax import lax
from jax.experimental import pallas as pl
from jax.experimental.pallas import tpu as pltpu
from jax.sharding import PartitionSpec as P

EPSILON = 1e-6
MSCALE = 0.1 * math.log(40.0) + 1.0
MESH = pl.DeviceIdType.MESH


OUT_W = 512
PIECE = 256
SLOTS = 4
EARLY = 2
HEAD_BLOCK = 8
SWAP_BLOCK = 16
NT = (((1,), (1,)), ((), ()))
NN = (((1,), (0,)), ((), ()))


GROUP = 8
BUFFERS = 3
CHUNK = 128


def attend_kernel(score_scale, len_ref, abs_hbm, pe_hbm, new_ref, pe_new_ref, ckv_ref, kpe_ref, wuv_ref,
                  out_ref, new_out_ref, pe_out_ref, order_buf, turned_buf, abs_ref, pe_ref, kv_buf, kp_buf, lat_buf, wuv_buf, kv_sem, kp_sem, wuv_sem, query_sem):
    query_copies = [pltpu.make_async_copy(abs_hbm, abs_ref, query_sem.at[0]), pltpu.make_async_copy(pe_hbm, pe_ref, query_sem.at[1])]
    for made in query_copies:
        made.start()
    rows, heads, latent_dim = abs_ref.shape
    seq = ckv_ref.shape[1]
    variants = seq // CHUNK
    groups = rows // GROUP
    value_dim = wuv_ref.shape[2]

    def chunks_of(row):
        return len_ref[row] // CHUNK

    def count_step(row, tally):
        return tuple(count + (chunks_of(row) == which).astype(jnp.int32) for which, count in enumerate(tally))

    tally = lax.fori_loop(0, rows, count_step, (jnp.int32(0),) * variants)
    starts = [jnp.int32(0)]
    for which in range(variants - 1):
        starts.append(starts[-1] + tally[which])

    def place_step(row, heads_of):
        mine = [chunks_of(row) == which for which in range(variants)]
        place = sum(jnp.where(hit, head, 0) for hit, head in zip(mine, heads_of))
        order_buf[place] = row
        return tuple(head + hit.astype(jnp.int32) for hit, head in zip(mine, heads_of))

    lax.fori_loop(0, rows, place_step, tuple(starts))

    def group_chunks(group):
        return chunks_of(order_buf[group * GROUP + GROUP - 1]) + 1

    def copies(group, size):
        slot = lax.rem(group, BUFFERS)
        made = []
        for place in range(GROUP):
            row = order_buf[group * GROUP + place]
            made.append(pltpu.make_async_copy(ckv_ref.at[row, pl.ds(0, size), :], kv_buf.at[slot, place, pl.ds(0, size), :], kv_sem.at[slot, place]))
            made.append(pltpu.make_async_copy(kpe_ref.at[row, :, pl.ds(0, size)], kp_buf.at[slot, place, :, pl.ds(0, size)], kp_sem.at[slot, place]))
        return made

    def start(group):
        for count in range(1, variants + 1):
            @pl.when(group_chunks(group) == count)
            def _():
                for made in copies(group, count * CHUNK):
                    made.start()

    for group in range(BUFFERS - 1):
        start(group)
    wuv_copy = pltpu.make_async_copy(wuv_ref, wuv_buf, wuv_sem)
    wuv_copy.start()
    turned_buf[...] = pe_new_ref[...].astype(jnp.float32).T
    new_out_ref[...] = new_ref[...]
    pe_out_ref[...] = pe_new_ref[...]

    def compute(group, size):
        slot = lax.rem(group, BUFFERS)
        for made in copies(group, size):
            made.wait()
        rows_of = [order_buf[group * GROUP + place] for place in range(GROUP)]
        for place, row in enumerate(rows_of):
            length = len_ref[row]
            base = pl.multiple_of((row // 16) * 16, 16)
            picked = new_ref[pl.ds(base, 16), :].astype(jnp.float32)
            hit = lax.broadcasted_iota(jnp.int32, picked.shape, 0) == row - base
            new = jnp.sum(jnp.where(hit, picked, 0.0), axis=0, keepdims=True)
            hit = lax.broadcasted_iota(jnp.int32, turned_buf.shape, 1) == row
            new_pe = jnp.sum(jnp.where(hit, turned_buf[...], 0.0), axis=1, keepdims=True)
            base = pl.multiple_of((length // 16) * 16, 16)
            block = kv_buf[slot, place, pl.ds(base, 16), :]
            hit = lax.broadcasted_iota(jnp.int32, block.shape, 0) == length - base
            kv_buf[slot, place, pl.ds(base, 16), :] = jnp.where(hit, new, block.astype(jnp.float32)).astype(jnp.bfloat16)
            lane = pl.multiple_of((length // CHUNK) * CHUNK, CHUNK)
            block = kp_buf[slot, place, :, pl.ds(lane, CHUNK)]
            hit = lax.broadcasted_iota(jnp.int32, block.shape, 1) == length - lane
            kp_buf[slot, place, :, pl.ds(lane, CHUNK)] = jnp.where(hit, new_pe, block.astype(jnp.float32)).astype(jnp.bfloat16)
        all_scores = [(lax.dot_general(abs_ref[row], kv_buf[slot, place, :size, :], NT, preferred_element_type=jnp.float32)
                       + jnp.dot(pe_ref[row], kp_buf[slot, place, :, :size], preferred_element_type=jnp.float32)) * score_scale
                      for place, row in enumerate(rows_of)]
        weights = []
        for place, row in enumerate(rows_of):
            positions = lax.broadcasted_iota(jnp.int32, (heads, size), 1)
            scores = jnp.where(positions <= len_ref[row], all_scores[place], -jnp.inf)
            exp_all = jnp.exp(scores - jnp.max(scores, axis=1, keepdims=True))
            weights.append((exp_all.astype(jnp.bfloat16), jnp.sum(exp_all, axis=1, keepdims=True)))
        for place, row in enumerate(rows_of):
            weighted = jnp.dot(weights[place][0], kv_buf[slot, place, :size, :], preferred_element_type=jnp.float32)
            lat_buf[row] = (weighted / weights[place][1]).astype(jnp.bfloat16)

    def group_step(group, carry):
        @pl.when(group + BUFFERS - 1 < groups)
        def _():
            start(group + BUFFERS - 1)
        for count in range(1, variants + 1):
            @pl.when(group_chunks(group) == count)
            def _():
                compute(group, count * CHUNK)
        return carry

    for made in query_copies:
        made.wait()
    lax.fori_loop(0, groups, group_step, 0)
    wuv_copy.wait()

    def value_step(block, carry):
        sel = pl.ds(pl.multiple_of(block * SWAP_BLOCK, SWAP_BLOCK), SWAP_BLOCK)
        lat = jnp.swapaxes(lat_buf[:, sel, :], 0, 1)
        wuv = jnp.swapaxes(wuv_buf[:, sel, :], 0, 1)
        for head in range(SWAP_BLOCK):
            dst = pl.ds(pl.multiple_of(block * SWAP_BLOCK * value_dim + head * value_dim, value_dim), value_dim)
            out_ref[:, dst] = jnp.dot(lat[head], wuv[head], preferred_element_type=jnp.float32).astype(jnp.bfloat16)
        return carry

    lax.fori_loop(0, heads // SWAP_BLOCK, value_step, 0)


def attend(q_abs, q_pe, ckv_new, kpe_new, ckv_cache, kpe_cache, cache_len, w_uv, score_scale):
    rows, heads, latent_dim = q_abs.shape
    rope_dim = q_pe.shape[2]
    seq = ckv_cache.shape[1]
    value_dim = w_uv.shape[2]
    smem = pl.BlockSpec(memory_space=pltpu.SMEM)
    vmem = pl.BlockSpec(memory_space=pltpu.VMEM)
    anywhere = pl.BlockSpec(memory_space=pl.ANY)
    dma = pltpu.SemaphoreType.DMA
    return pl.pallas_call(
        functools.partial(attend_kernel, score_scale),
        out_shape=[jax.ShapeDtypeStruct((rows, heads * value_dim), jnp.bfloat16),
                   jax.ShapeDtypeStruct(ckv_new.shape, jnp.bfloat16), jax.ShapeDtypeStruct(kpe_new.shape, jnp.bfloat16)],
        in_specs=[smem, anywhere, anywhere, vmem, vmem, anywhere, anywhere, anywhere],
        out_specs=[vmem, vmem, vmem],
        scratch_shapes=[
            pltpu.SMEM((rows,), jnp.int32),
            pltpu.VMEM((rope_dim, rows), jnp.float32),
            pltpu.VMEM(q_abs.shape, jnp.bfloat16),
            pltpu.VMEM(q_pe.shape, jnp.bfloat16),
            pltpu.VMEM((BUFFERS, GROUP, seq, latent_dim), jnp.bfloat16),
            pltpu.VMEM((BUFFERS, GROUP, rope_dim, seq), jnp.bfloat16),
            pltpu.VMEM((rows, heads, latent_dim), jnp.bfloat16),
            pltpu.VMEM(w_uv.shape, jnp.bfloat16),
            dma((BUFFERS, GROUP)), dma((BUFFERS, GROUP)), dma(()), dma((2,)),
        ],
        compiler_params=pltpu.CompilerParams(vmem_limit_bytes=60 * 1000 * 1000),
        name='attend',
    )(cache_len, q_abs, q_pe, ckv_new, kpe_new, ckv_cache, jnp.swapaxes(kpe_cache, 1, 2), w_uv)


DQ_W = 256


def _sides():
    rep = lax.axis_index('rep')
    me = lax.axis_index('dp')
    chip = me // 2
    core = lax.rem(me, 2)
    return rep, me, chip, core


def front_kernel(x_ref, gain_ref, gain_q_ref, gain_kv_ref, cos_ref, sin_ref, wdq_ref, wdkv_ref, wuq_ref, wuk_ref,
                 abs_ref, pe_ref, ckv_ref, kpe_ref,
                 dq_buf, dkv_buf, uq_buf, uk_buf, x_recv, cs_recv, a_chip, cq_raw, cq_chip, kv_part, kv_recv, abs_part, pe_part, stat,
                 dq_sem, dkv_sem, uq_sem, uk_sem, in_send, in_recv, cq_send, cq_recv, kv_send, kv_got, abs_send, abs_recv, pe_send, pe_recv, keep_sem):
    rep, me, chip, core = _sides()
    part = chip * 2 + (1 - core)
    rows, d_model = x_ref.shape
    latent_dim = ckv_ref.shape[1]
    rope_dim = kpe_ref.shape[1]
    half_dim = rope_dim // 2
    nope_dim = wuk_ref.shape[2]
    head_dim = nope_dim + rope_dim
    half_k = d_model // 2
    n_dq = dq_buf.shape[0]
    n_uq = uq_buf.shape[0]
    q_rank = cq_chip.shape[1]
    block_rows = HEAD_BLOCK * head_dim
    my_heads = n_uq * HEAD_BLOCK

    def dq_copy(index):
        cols = pl.ds(pl.multiple_of((core * n_dq + index) * DQ_W, DQ_W), DQ_W)
        return pltpu.make_async_copy(wdq_ref.at[:, cols], dq_buf.at[index], dq_sem.at[index])

    def uq_copy(index):
        sel = pl.ds(pl.multiple_of((core * n_uq + index) * block_rows, block_rows), block_rows)
        return pltpu.make_async_copy(wuq_ref.at[sel, :], uq_buf.at[index], uq_sem.at[index])

    my_k = pl.ds(pl.multiple_of(core * half_k, half_k), half_k)
    dkv_copy = pltpu.make_async_copy(wdkv_ref.at[:, my_k], dkv_buf, dkv_sem)
    heads_here = pl.ds(pl.multiple_of(core * my_heads, my_heads), my_heads)
    uk_copy = pltpu.make_async_copy(wuk_ref.at[:, heads_here, :], uk_buf, uk_sem)
    for index in range(n_dq):
        dq_copy(index).start()
    dkv_copy.start()
    uk_copy.start()
    for index in range(n_uq):
        uq_copy(index).start()

    barrier = pltpu.get_barrier_semaphore()
    pl.semaphore_signal(barrier, inc=1, device_id=(rep, part), device_id_type=MESH)
    pl.semaphore_wait(barrier, 1)

    def remote(src, dst, send, recv):
        return pltpu.make_async_remote_copy(src_ref=src, dst_ref=dst, send_sem=send, recv_sem=recv,
                                            device_id=(rep, part), device_id_type=MESH)

    swaps = [remote(x_ref, x_recv, in_send.at[0], in_recv.at[0]),
             remote(cos_ref, cs_recv.at[0], in_send.at[1], in_recv.at[1]),
             remote(sin_ref, cs_recv.at[1], in_send.at[2], in_recv.at[2])]
    for swap in swaps:
        swap.start()

    own = pl.ds(pl.multiple_of(core * rows, rows), rows)
    other = pl.ds(pl.multiple_of((1 - core) * rows, rows), rows)
    n_cols = d_model // OUT_W

    def normalise(src_ref, dst_rows):
        def square_step(index, total_sq):
            vals = src_ref[:, pl.ds(pl.multiple_of(index * OUT_W, OUT_W), OUT_W)].astype(jnp.float32)
            return total_sq + jnp.sum(vals * vals, axis=-1, keepdims=True)

        total_sq = lax.fori_loop(0, n_cols, square_step, jnp.zeros((rows, 1), jnp.float32))
        stat[...] = lax.rsqrt(total_sq * (1.0 / d_model) + EPSILON)

        def scale_step(index, carry):
            cols = pl.ds(pl.multiple_of(index * OUT_W, OUT_W), OUT_W)
            vals = src_ref[:, cols].astype(jnp.float32) * stat[...] * gain_ref[0:1, cols]
            a_chip[dst_rows, cols] = vals.astype(jnp.bfloat16)
            return carry

        lax.fori_loop(0, n_cols, scale_step, 0)

    normalise(x_ref, own)
    for swap in swaps:
        swap.wait()
    normalise(x_recv, other)

    def cq_copy(index):
        blk = cq_raw.at[core * n_dq + index]
        return remote(blk, blk, cq_send.at[index], cq_recv.at[index])

    def dq_step(index, carry):
        dq_copy(index).wait()
        cq_raw[core * n_dq + index] = jnp.dot(a_chip[...], dq_buf[index], preferred_element_type=jnp.float32)
        cq_copy(index).start()
        return carry

    lax.fori_loop(0, n_dq, dq_step, 0)

    dkv_copy.wait()
    kv_part[...] = lax.dot_general(a_chip[:, my_k], dkv_buf[...], NT, preferred_element_type=jnp.float32)
    kv_copy = remote(kv_part.at[other, :], kv_recv, kv_send, kv_got)
    kv_copy.start()

    for index in range(n_dq):
        cq_copy(index).wait()
    total_sq = jnp.zeros((2 * rows, 1), jnp.float32)
    for index in range(2 * n_dq):
        vals = cq_raw[index]
        total_sq += jnp.sum(vals * vals, axis=-1, keepdims=True)
    inv = lax.rsqrt(total_sq * (1.0 / q_rank) + EPSILON)
    for index in range(2 * n_dq):
        for lane in range(0, DQ_W, 128):
            start = index * DQ_W + lane
            gain = gain_q_ref[start // 128:start // 128 + 1, :]
            cq_chip[:, start:start + 128] = (cq_raw[index, :, lane:lane + 128] * inv * gain).astype(jnp.bfloat16)

    cos_own, sin_own = cos_ref[...].T, sin_ref[...].T
    cos_far, sin_far = cs_recv[0].T, cs_recv[1].T
    first = core == 0
    cos_t = jnp.concatenate([jnp.where(first, cos_own, cos_far), jnp.where(first, cos_far, cos_own)], axis=0)
    sin_t = jnp.concatenate([jnp.where(first, sin_own, sin_far), jnp.where(first, sin_far, sin_own)], axis=0)
    uk_copy.wait()

    def head_cols(index):
        return pl.ds(pl.multiple_of(core * my_heads + index * SWAP_BLOCK, SWAP_BLOCK), SWAP_BLOCK)

    def abs_copy(index):
        return remote(abs_part.at[index, other], abs_ref.at[:, head_cols(index), :], abs_send.at[index], abs_recv.at[index])

    def pe_copy(index):
        return remote(pe_part.at[index, other], pe_ref.at[:, head_cols(index), :], pe_send.at[index], pe_recv.at[index])

    def abs_keep(index):
        return pltpu.make_async_copy(abs_part.at[index, own], abs_ref.at[:, head_cols(index), :], keep_sem.at[0, index])

    def pe_keep(index):
        return pltpu.make_async_copy(pe_part.at[index, own], pe_ref.at[:, head_cols(index), :], keep_sem.at[1, index])

    per_swap = SWAP_BLOCK // HEAD_BLOCK

    def uq_step(index, carry):
        absorbed = []
        turned = []
        for sub in range(per_swap):
            uq_copy(index * per_swap + sub).wait()
        wuk = jnp.swapaxes(uk_buf[:, pl.ds(pl.multiple_of(index * SWAP_BLOCK, SWAP_BLOCK), SWAP_BLOCK), :], 0, 1)
        for sub in range(per_swap):
            q_val = lax.dot_general(cq_chip[...], uq_buf[index * per_swap + sub], NT, preferred_element_type=jnp.float32)
            for head in range(HEAD_BLOCK):
                base = head * head_dim
                nope = q_val[:, base:base + nope_dim].astype(jnp.bfloat16)
                low_half = q_val[:, base + nope_dim:base + nope_dim + half_dim]
                high_half = q_val[:, base + nope_dim + half_dim:base + head_dim]
                turned.append(jnp.concatenate([low_half * cos_t - high_half * sin_t, high_half * cos_t + low_half * sin_t], axis=1).astype(jnp.bfloat16))
                absorbed.append(lax.dot_general(nope, wuk[sub * HEAD_BLOCK + head], NT, preferred_element_type=jnp.float32).astype(jnp.bfloat16))
        abs_part[index] = jnp.swapaxes(jnp.stack(absorbed, axis=0), 0, 1)
        pe_part[index] = jnp.swapaxes(jnp.stack(turned, axis=0), 0, 1)
        for move in (abs_copy, pe_copy, abs_keep, pe_keep):
            move(index).start()
        return carry

    n_swap = n_uq // per_swap
    lax.fori_loop(0, n_swap, uq_step, 0)

    kv_copy.wait()
    kv_val = kv_part[own, :] + kv_recv[...]
    latent = kv_val[:, :latent_dim]
    inv = lax.rsqrt(jnp.mean(latent * latent, axis=-1, keepdims=True) + EPSILON)
    ckv_ref[...] = (latent * inv * gain_kv_ref[...]).astype(jnp.bfloat16)
    low_half = kv_val[:, latent_dim:latent_dim + half_dim]
    high_half = kv_val[:, latent_dim + half_dim:]
    kpe_ref[...] = jnp.concatenate([low_half * cos_own - high_half * sin_own, high_half * cos_own + low_half * sin_own], axis=1).astype(jnp.bfloat16)
    for index in range(n_swap):
        for move in (abs_copy, pe_copy, abs_keep, pe_keep):
            move(index).wait()


def front(hidden, norm_attn, w_dq, norm_q, w_uq, w_dkv, norm_kv, w_uk, rope_cos, rope_sin):
    rows, d_model = hidden.shape
    latent_dim, heads, nope_dim = w_uk.shape
    q_rank, _, head_dim = w_uq.shape
    rope_dim = head_dim - nope_dim
    half_dim = rope_dim // 2
    kv_dim = w_dkv.shape[1]
    n_dq = q_rank // 2 // DQ_W
    n_uq = heads // 2 // HEAD_BLOCK
    n_swap = heads // 2 // SWAP_BLOCK
    f32, bf16 = jnp.float32, jnp.bfloat16
    vmem = pl.BlockSpec(memory_space=pltpu.VMEM)
    anywhere = pl.BlockSpec(memory_space=pl.ANY)
    dma = pltpu.SemaphoreType.DMA
    return pl.pallas_call(
        front_kernel,
        out_shape=[
            jax.ShapeDtypeStruct((rows, heads, latent_dim), bf16),
            jax.ShapeDtypeStruct((rows, heads, rope_dim), bf16),
            jax.ShapeDtypeStruct((rows, latent_dim), bf16),
            jax.ShapeDtypeStruct((rows, rope_dim), bf16),
        ],
        in_specs=[vmem] * 6 + [anywhere] * 4,
        out_specs=[anywhere, anywhere, vmem, vmem],
        scratch_shapes=[
            pltpu.VMEM((n_dq, d_model, DQ_W), bf16),
            pltpu.VMEM((kv_dim, d_model // 2), bf16),
            pltpu.VMEM((n_uq, HEAD_BLOCK * head_dim, q_rank), bf16),
            pltpu.VMEM((latent_dim, heads // 2, nope_dim), bf16),
            pltpu.VMEM((rows, d_model), bf16),
            pltpu.VMEM((2, half_dim, rows), f32),
            pltpu.VMEM((2 * rows, d_model), bf16),
            pltpu.VMEM((2 * n_dq, 2 * rows, DQ_W), f32),
            pltpu.VMEM((2 * rows, q_rank), bf16),
            pltpu.VMEM((2 * rows, kv_dim), f32),
            pltpu.VMEM((rows, kv_dim), f32),
            pltpu.VMEM((n_swap, 2 * rows, SWAP_BLOCK, latent_dim), bf16),
            pltpu.VMEM((n_swap, 2 * rows, SWAP_BLOCK, rope_dim), bf16),
            pltpu.VMEM((rows, 1), f32),
            dma((n_dq,)), dma(()), dma((n_uq,)), dma(()), dma((3,)), dma((3,)), dma((n_dq,)), dma((n_dq,)), dma(()), dma(()),
            dma((n_swap,)), dma((n_swap,)), dma((n_swap,)), dma((n_swap,)), dma((2, n_swap)),
        ],
        compiler_params=pltpu.CompilerParams(collective_id=1, has_side_effects=True, vmem_limit_bytes=66 * 1000 * 1000),
        name='front',
    )(hidden, norm_attn.reshape(1, -1), norm_q.reshape(-1, 128), norm_kv.reshape(1, -1), rope_cos.T, rope_sin.T,
      w_dq, w_dkv.T, jnp.transpose(w_uq, (1, 2, 0)).reshape(heads * head_dim, q_rank), w_uk)


def attention_rows(hidden, ckv_cache, kpe_cache, cache_len, rope_cos, rope_sin, norm_attn, w_dq, norm_q, w_uq, w_dkv, norm_kv, w_uk, w_uv):
    score_scale = MSCALE * MSCALE / math.sqrt(w_uq.shape[2])
    q_abs, q_pe, ckv_new, kpe_new = front(hidden, norm_attn, w_dq, norm_q, w_uq, w_dkv, norm_kv, w_uk, rope_cos, rope_sin)
    head_out, ckv_new, kpe_new = attend(q_abs, q_pe, ckv_new, kpe_new, ckv_cache, kpe_cache, cache_len, w_uv, score_scale)
    return head_out, ckv_new, kpe_new


def tail_kernel(o_ref, x_ref, gain_ref, wout_ref, wgate_ref, wup_ref, wdown_ref, out_ref,
                slots, o_chip, x_chip, x_own, r_all, u_all, gate_buf, up_buf, act, sq_acc, pair_send, pair_recv, far_send, far_recv, own_sum,
                slot_sem, in_send, in_recv, loc_sem, rp_send, rp_recv, rx_send, rx_recv, rf_send, rf_recv,
                pp_send, pp_recv, px_send, px_recv):
    rep, me, chip, core = _sides()
    part = chip * 2 + (1 - core)
    opp = (1 - chip) * 2 + core
    diag = (1 - chip) * 2 + (1 - core)
    attn_k = wout_ref.shape[0]
    d_model = wgate_ref.shape[0]
    ff = wgate_ref.shape[1]
    rows = x_ref.shape[0]
    half = d_model // 2
    n_out = half // OUT_W
    n_ff = ff // OUT_W
    n_down = d_model // OUT_W
    first_ff = n_out
    first_down = n_out + 2 * n_ff
    total = first_down + n_down
    pieces = OUT_W // PIECE
    n_half = half // PIECE
    n_all = d_model // PIECE

    def col(index):
        return pl.ds(pl.multiple_of(index * OUT_W, OUT_W), OUT_W)

    def piece(index):
        return pl.ds(pl.multiple_of(index * PIECE, PIECE), PIECE)

    def row_block(owner, count=1):
        return pl.ds(pl.multiple_of(owner * rows, rows), count * rows)

    def slot_copy(kind, index, step):
        slot = lax.rem(step, SLOTS)
        src = {'out': wout_ref, 'gate': wgate_ref, 'up': wup_ref, 'down': wdown_ref}[kind]
        depth = src.shape[0]
        return pltpu.make_async_copy(src.at[:, col(index)], slots.at[slot, pl.ds(0, depth), :], slot_sem.at[slot])

    def fetch(step):
        @pl.when(step < first_ff)
        def _():
            slot_copy('out', core * n_out + step, step).start()

        @pl.when((step >= first_ff) & (step < first_down) & (lax.rem(step - first_ff, 2) == 0))
        def _():
            slot_copy('gate', (step - first_ff) // 2, step).start()

        @pl.when((step >= first_ff) & (step < first_down) & (lax.rem(step - first_ff, 2) == 1))
        def _():
            slot_copy('up', (step - first_ff) // 2, step).start()

        @pl.when((step >= first_down) & (step < total))
        def _():
            slot_copy('down', step - first_down, step).start()

    my_rows = row_block(core)
    my_half = pl.ds(pl.multiple_of(core * half, half), half)
    their_half = pl.ds(pl.multiple_of((1 - core) * half, half), half)
    keep_o = pltpu.make_async_copy(o_ref, o_chip.at[my_rows, :], loc_sem.at[0])
    keep_x = pltpu.make_async_copy(x_ref.at[:, my_half], x_chip.at[my_rows, :], loc_sem.at[1])
    give_x = pltpu.make_async_copy(x_ref.at[:, their_half], x_own, loc_sem.at[2])
    keep_o.start()
    give_x.start()
    keep_x.start()
    slot_copy('out', core * n_out, 0).start()

    barrier = pltpu.get_barrier_semaphore()
    for peer in (part, opp):
        pl.semaphore_signal(barrier, inc=1, device_id=(rep, peer), device_id_type=MESH)
    pl.semaphore_wait(barrier, 2)

    def remote(src, dst, send, recv, peer):
        return pltpu.make_async_remote_copy(src_ref=src, dst_ref=dst, send_sem=send, recv_sem=recv,
                                            device_id=(rep, peer), device_id_type=MESH)

    keep_o.wait()
    send_o = remote(o_chip.at[my_rows, :], o_chip.at[my_rows, :], in_send.at[0], in_recv.at[0], part)
    send_o.start()
    give_x.wait()
    send_x = remote(x_own, x_chip.at[my_rows, :], in_send.at[1], in_recv.at[1], part)
    send_x.start()
    for step in range(1, SLOTS):
        slot_copy('out', core * n_out + step, step).start()
    sq_acc[...] = jnp.zeros_like(sq_acc)
    gate_buf[...] = jnp.zeros_like(gate_buf)
    up_buf[...] = jnp.zeros_like(up_buf)
    keep_x.wait()
    send_o.wait()
    send_x.wait()

    chip_rows = row_block(chip * 2, 2)
    far_rows = row_block((1 - chip) * 2, 2)

    def r_pair(index):
        blk = r_all.at[core * n_half + index, chip_rows, :]
        return remote(blk, blk, rp_send.at[index], rp_recv.at[index], part)

    def r_far(index):
        blk = r_all.at[core * n_half + index, chip_rows, :]
        return remote(blk, blk, rx_send.at[index], rx_recv.at[index], opp)

    def r_forward(index):
        blk = r_all.at[core * n_half + index, far_rows, :]
        return remote(blk, blk, rf_send.at[index], rf_recv.at[index], part)

    def add_squares(sel, vals):
        wide = vals.astype(jnp.float32)
        wide = wide * wide
        acc = sq_acc[sel, :]
        for lane in range(0, PIECE, 128):
            acc = acc + wide[:, lane:lane + 128]
        sq_acc[sel, :] = acc

    def take_pair(index):
        r_pair(index).wait_recv()
        add_squares(chip_rows, r_all[(1 - core) * n_half + index, chip_rows, :])

    def take_far(index):
        r_far(index).wait_recv()
        r_forward(index).start()
        add_squares(far_rows, r_all[core * n_half + index, far_rows, :])

    def take_forward(index):
        r_forward(index).wait_recv()
        add_squares(far_rows, r_all[(1 - core) * n_half + index, far_rows, :])

    lags = ((take_pair, 2), (take_far, 4), (take_forward, 6))

    def out_step(index, carry):
        slot_copy('out', core * n_out + index, index).wait()
        for sub in range(pieces):
            here = index * pieces + sub
            acc = jnp.dot(o_chip[...], slots[lax.rem(index, SLOTS), :attn_k, sub * PIECE:(sub + 1) * PIECE], preferred_element_type=jnp.float32)
            vals = (x_chip[:, piece(here)].astype(jnp.float32) + acc).astype(jnp.bfloat16)
            r_all[core * n_half + here, chip_rows, :] = vals
            r_far(here).start()
            r_pair(here).start()
            add_squares(chip_rows, vals)
            for take, lag in lags:
                @pl.when(here >= lag)
                def _(take=take, lag=lag):
                    take(here - lag)
        fetch(index + SLOTS)
        return carry

    lax.fori_loop(0, n_out, out_step, 0)

    def inverse(owner):
        total_sq = jnp.sum(sq_acc[row_block(owner), :], axis=-1, keepdims=True)
        return lax.rsqrt(total_sq * (1.0 / d_model) + EPSILON)

    def normalise(places):
        invs = [inverse(owner) for _, owner in places]

        def norm_step(index, carry):
            for (place, owner), inv in zip(places, carry):
                vals = r_all[index, row_block(owner), :].astype(jnp.float32) * inv * gain_ref[0:1, piece(index)]
                u_all[place * rows:(place + 1) * rows, piece(index)] = vals.astype(jnp.bfloat16)
            return carry

        lax.fori_loop(0, n_all, norm_step, tuple(invs))

    for index in range(n_half - 2, n_half):
        take_pair(index)
    take_far(n_half - 4)
    take_forward(n_half - 6)
    take_far(n_half - 3)
    take_forward(n_half - 5)
    normalise(((0, part), (1, me)))
    near = slice(0, 2 * rows)
    far = slice(2 * rows, 4 * rows)

    def activate(gate_val, up_val):
        return (gate_val * jax.nn.sigmoid(gate_val) * up_val).astype(jnp.bfloat16)

    def product(sel, step):
        return jnp.dot(u_all[sel, :], slots[lax.rem(step, SLOTS), :d_model, :], preferred_element_type=jnp.float32)

    def early(index, sel):
        step = first_ff + 2 * index
        gate_val = product(sel, step)
        act[sel, index * OUT_W:(index + 1) * OUT_W] = activate(gate_val, product(sel, step + 1))

    for index in range(EARLY):
        slot_copy('gate', index, first_ff + 2 * index).wait()
        slot_copy('up', index, first_ff + 2 * index + 1).wait()
        early(index, near)
        if index == 0:
            take_far(n_half - 2)
            take_far(n_half - 1)
            take_forward(n_half - 4)
            take_forward(n_half - 3)
    take_forward(n_half - 2)
    take_forward(n_half - 1)
    normalise(((2, diag), (3, opp)))
    for index in range(EARLY):
        early(index, far)
        fetch(first_ff + 2 * index + SLOTS)
        fetch(first_ff + 2 * index + 1 + SLOTS)

    def ff_step(index, carry):
        step = first_ff + 2 * index
        now, before = lax.rem(index, 2), lax.rem(index + 1, 2)
        slot_copy('gate', index, step).wait()
        act[:, col(jnp.maximum(index - 1, EARLY))] = activate(gate_buf[before], up_buf[...])
        gate_buf[now] = product(slice(None), step)
        fetch(step + SLOTS)
        slot_copy('up', index, step + 1).wait()
        up_buf[...] = product(slice(None), step + 1)
        fetch(step + 1 + SLOTS)
        return carry

    lax.fori_loop(EARLY, n_ff, ff_step, 0)
    act[:, (n_ff - 1) * OUT_W:] = activate(gate_buf[(n_ff - 1) % 2], up_buf[...])

    def pair_copy(index):
        return remote(pair_send.at[index], pair_recv.at[index], pp_send.at[index], pp_recv.at[index], part)

    def far_copy(index):
        return remote(far_send.at[index], far_recv.at[index], px_send.at[index], px_recv.at[index], opp)

    def combine(index):
        pair_copy(index).wait_recv()
        far_send[index] += pair_recv[index, rows:, :]
        far_copy(index).start()
        own_sum[index] += pair_recv[index, :rows, :]

    def down_step(index, carry):
        step = first_down + index
        slot_copy('down', index, step).wait()
        for sub in range(pieces):
            here = index * pieces + sub
            part_sum = jnp.dot(act[...], slots[lax.rem(step, SLOTS), :ff, sub * PIECE:(sub + 1) * PIECE], preferred_element_type=jnp.float32)
            pair_send[here, :rows] = part_sum[:rows]
            pair_send[here, rows:] = part_sum[2 * rows:3 * rows]
            own_sum[here] = part_sum[rows:2 * rows]
            far_send[here] = part_sum[3 * rows:]
            pair_copy(here).start()

            @pl.when(here >= 1)
            def _():
                combine(here - 1)
        fetch(step + SLOTS)
        return carry

    lax.fori_loop(0, n_down, down_step, 0)
    combine(n_all - 1)

    def settle(index, carry):
        r_pair(index).wait_send()
        r_far(index).wait_send()
        r_forward(index).wait_send()
        return carry

    lax.fori_loop(0, n_half, settle, 0)
    own_rows = row_block(me)

    def finish(index, carry):
        far_copy(index).wait()
        pair_copy(index).wait_send()
        mlp = own_sum[index] + far_recv[index]
        out_ref[:, piece(index)] = (r_all[index, own_rows, :].astype(jnp.float32) + mlp).astype(jnp.bfloat16)
        return carry

    lax.fori_loop(0, n_all, finish, 0)


def tail(head_out, hidden, norm_mlp, w_out, w_gate, w_up, w_down):
    rows, d_model = hidden.shape
    attn_k = w_out.shape[0]
    ff = w_gate.shape[1]
    n_half = d_model // 2 // PIECE
    n_all = d_model // PIECE
    depth = max(attn_k, d_model, ff)
    vmem = pl.BlockSpec(memory_space=pltpu.VMEM)
    anywhere = pl.BlockSpec(memory_space=pl.ANY)
    dma = pltpu.SemaphoreType.DMA
    f32, bf16 = jnp.float32, jnp.bfloat16
    return pl.pallas_call(
        tail_kernel,
        out_shape=jax.ShapeDtypeStruct((rows, d_model), bf16),
        in_specs=[anywhere, anywhere, vmem, anywhere, anywhere, anywhere, anywhere],
        out_specs=vmem,
        scratch_shapes=[
            pltpu.VMEM((SLOTS, depth, OUT_W), bf16),
            pltpu.VMEM((2 * rows, attn_k), bf16),
            pltpu.VMEM((2 * rows, d_model // 2), bf16),
            pltpu.VMEM((rows, d_model // 2), bf16),
            pltpu.VMEM((n_all, 4 * rows, PIECE), bf16),
            pltpu.VMEM((4 * rows, d_model), bf16),
            pltpu.VMEM((2, 4 * rows, OUT_W), f32),
            pltpu.VMEM((4 * rows, OUT_W), f32),
            pltpu.VMEM((4 * rows, ff), bf16),
            pltpu.VMEM((4 * rows, 128), f32),
            pltpu.VMEM((n_all, 2 * rows, PIECE), f32),
            pltpu.VMEM((n_all, 2 * rows, PIECE), f32),
            pltpu.VMEM((n_all, rows, PIECE), f32),
            pltpu.VMEM((n_all, rows, PIECE), f32),
            pltpu.VMEM((n_all, rows, PIECE), f32),
            dma((SLOTS,)), dma((2,)), dma((2,)), dma((3,)),
            dma((n_half,)), dma((n_half,)), dma((n_half,)), dma((n_half,)), dma((n_half,)), dma((n_half,)),
            dma((n_all,)), dma((n_all,)), dma((n_all,)), dma((n_all,)),
        ],
        compiler_params=pltpu.CompilerParams(collective_id=0, has_side_effects=True, vmem_limit_bytes=66 * 1000 * 1000),
        name='tail',
    )(head_out, hidden, norm_mlp.reshape(1, d_model), w_out, w_gate, w_up, w_down)


def solution(mesh):
    row_spec = P(('rep', 'dp'), None)
    cube_spec = P(('rep', 'dp'), None, None)
    full_spec = P()
    in_specs = (row_spec, cube_spec, cube_spec, P(('rep', 'dp')), row_spec, row_spec,
                full_spec, full_spec, full_spec, full_spec, full_spec, full_spec, full_spec, full_spec, full_spec, full_spec,
                P(None, 'dp'), P(None, 'dp'), P('dp', None))

    def local_step(hidden, ckv_cache, kpe_cache, cache_len, rope_cos, rope_sin, norm_attn, w_dq, norm_q, w_uq, w_dkv, norm_kv, w_uk, w_uv, w_out, norm_mlp, w_gate, w_up, w_down):
        head_out, ckv_new, kpe_new = attention_rows(hidden, ckv_cache, kpe_cache, cache_len, rope_cos, rope_sin, norm_attn, w_dq, norm_q, w_uq, w_dkv, norm_kv, w_uk, w_uv)
        out_hidden = tail(head_out, hidden, norm_mlp, w_out.reshape(-1, w_out.shape[-1]), w_gate, w_up, w_down)
        return out_hidden, ckv_new, kpe_new

    return jax.shard_map(local_step, mesh=mesh, in_specs=in_specs, out_specs=(row_spec, row_spec, row_spec), check_vma=False)
```

profile of v0, /device:TPU:0, one launch (start us, length us, event | category | flops | bytes accessed | tf_op | source)
XLA Modules:
  0.0 171.6 jit_solution(16926149021336503361)
XLA Ops:
  0.6 26.2 %front.1 = (bf16[64,64,512]{2,1,0:T(8,128)(2,1)}, bf16[64,64,64]{2,1,0:T(8,128)(2,1)}, bf16[64,512]{1,0:T(8,128)(2,1)}, bf16[64,64]{1,0:T(8,128)(2,1)}) custom-call(bf16[64,7168]{1,0:T(8,128)(2,1)} %x_ref.3, f32[1,7168]{1,0:T(1,128)} %bitcast.15, f32[12,128]{1,0:T(8,128)} %bitcast.19, f32[1,512]{1,0:T(1,128)} %bitcast.20, f32[32,64]{1,0:T(8,128)} %bitcast.17, ...), custom_call_target="tpu_custom_call" | custom-call | tf_op jit(solution)/shard_map/front/pallas_call | solution.py:372
  26.9 28.0 %attend.1 = (bf16[64,8192]{1,0:T(8,128)(2,1)}, bf16[64,512]{1,0:T(8,128)(2,1)}, bf16[64,64]{1,0:T(8,128)(2,1)}) custom-call(s32[64]{0:T(128)} %len_ref.1, bf16[64,64,512]{2,1,0:T(8,128)(2,1)} %get-tuple-element.10.abs_hbm, bf16[64,64,64]{2,1,0:T(8,128)(2,1)} %get-tuple-element.11.pe_hbm, bf16[64,512]{1,0:T(8,128)(2,1)} %get-tuple-element.12.new_ref, ...), custom_call_target="tpu_custom_call" | custom-call | tf_op jit(solution)/shard_map/attend/pallas_call | solution.py:157
  54.9 114.5 %tail.1 = bf16[64,7168]{1,0:T(8,128)(2,1)} custom-call(bf16[64,8192]{1,0:T(8,128)(2,1)} %get-tuple-element.14.o_ref, bf16[64,7168]{1,0:T(8,128)(2,1)} %x_ref.3, f32[1,7168]{1,0:T(1,128)} %bitcast.16, bf16[8192,7168]{1,0:T(8,128)(2,1)} %bitcast.10.wout_ref, bf16[7168,4608]{1,0:T(8,128)(2,1)} %wgate_ref.1, bf16[7168,4608]{1,0:T(8,128)(2,1)} %wup_ref.1, ...), custom_call_target="tpu_custom_call" | custom-call | tf_op jit(solution)/shard_map/tail/pallas_call | solution.py:691
  169.4 2.2 %copy.23 = bf16[64,7168]{1,0:T(8,128)(2,1)} copy(bf16[64,7168]{1,0:T(8,128)(2,1)} %tail.1) | data formatting | bytes 1835008
where the time goes:
time: 172 us
  Pallas kernels  169 us (98%)
  local copies, waits for them, and re-layouts  2.16 us (1%)
    pallas_call x1, Pallas kernels, tail(): pl.pallas_call(tail_kernel, out_shape=jax.ShapeDtypeStruct((rows, d_model...  115 us
    pallas_call x1, Pallas kernels, attend(): pl.pallas_call(functools.partial(attend_kernel, score_scale), out_shape=[...  28 us
    pallas_call x1, Pallas kernels, front(): pl.pallas_call(front_kernel, out_shape=[jax.ShapeDtypeStruct((rows, heads...  26.2 us

commit v1 on v0

--- a/solution.py
+++ b/solution.py
@@ -79,7 +79,6 @@
     for group in range(BUFFERS - 1):
         start(group)
     wuv_copy = pltpu.make_async_copy(wuv_ref, wuv_buf, wuv_sem)
-    wuv_copy.start()
     turned_buf[...] = pe_new_ref[...].astype(jnp.float32).T
     new_out_ref[...] = new_ref[...]
     pe_out_ref[...] = pe_new_ref[...]
@@ -119,6 +118,10 @@
             lat_buf[row] = (weighted / weights[place][1]).astype(jnp.bfloat16)
 
     def group_step(group, carry):
+        @pl.when(group == groups - 3)
+        def _():
+            wuv_copy.start()
+
         @pl.when(group + BUFFERS - 1 < groups)
         def _():
             start(group + BUFFERS - 1)
@@ -189,8 +192,8 @@
 
 def front_kernel(x_ref, gain_ref, gain_q_ref, gain_kv_ref, cos_ref, sin_ref, wdq_ref, wdkv_ref, wuq_ref, wuk_ref,
                  abs_ref, pe_ref, ckv_ref, kpe_ref,
-                 dq_buf, dkv_buf, uq_buf, uk_buf, x_recv, cs_recv, a_chip, cq_raw, cq_chip, kv_part, kv_recv, abs_part, pe_part, stat,
-                 dq_sem, dkv_sem, uq_sem, uk_sem, in_send, in_recv, cq_send, cq_recv, kv_send, kv_got, abs_send, abs_recv, pe_send, pe_recv, keep_sem):
+                 dq_buf, dkv_buf, uq_buf, uk_buf, wuk_buf, x_own, x_recv, cs_recv, a_chip, cq_raw, cq_chip, kv_part, kv_recv, abs_part, pe_part, stat,
+                 x_sem, dq_sem, dkv_sem, uq_sem, uk_sem, in_send, in_recv, cq_send, cq_recv, kv_send, kv_got, abs_send, abs_recv, pe_send, pe_recv, keep_sem):
     rep, me, chip, core = _sides()
     part = chip * 2 + (1 - core)
     rows, d_model = x_ref.shape
@@ -218,12 +221,9 @@
     dkv_copy = pltpu.make_async_copy(wdkv_ref.at[:, my_k], dkv_buf, dkv_sem)
     heads_here = pl.ds(pl.multiple_of(core * my_heads, my_heads), my_heads)
     uk_copy = pltpu.make_async_copy(wuk_ref.at[:, heads_here, :], uk_buf, uk_sem)
-    for index in range(n_dq):
-        dq_copy(index).start()
-    dkv_copy.start()
-    uk_copy.start()
-    for index in range(n_uq):
-        uq_copy(index).start()
+    x_copy = pltpu.make_async_copy(x_ref, x_own, x_sem)
+    x_copy.start()
+    dq_copy(0).start()
 
     barrier = pltpu.get_barrier_semaphore()
     pl.semaphore_signal(barrier, inc=1, device_id=(rep, part), device_id_type=MESH)
@@ -233,11 +233,18 @@
         return pltpu.make_async_remote_copy(src_ref=src, dst_ref=dst, send_sem=send, recv_sem=recv,
                                             device_id=(rep, part), device_id_type=MESH)
 
-    swaps = [remote(x_ref, x_recv, in_send.at[0], in_recv.at[0]),
+    x_copy.wait()
+    swaps = [remote(x_own, x_recv, in_send.at[0], in_recv.at[0]),
              remote(cos_ref, cs_recv.at[0], in_send.at[1], in_recv.at[1]),
              remote(sin_ref, cs_recv.at[1], in_send.at[2], in_recv.at[2])]
     for swap in swaps:
         swap.start()
+    for index in range(1, n_dq):
+        dq_copy(index).start()
+    uk_copy.start()
+    for index in range(n_uq):
+        uq_copy(index).start()
+    dkv_copy.start()
 
     own = pl.ds(pl.multiple_of(core * rows, rows), rows)
     other = pl.ds(pl.multiple_of((1 - core) * rows, rows), rows)
@@ -259,7 +266,7 @@
 
         lax.fori_loop(0, n_cols, scale_step, 0)
 
-    normalise(x_ref, own)
+    normalise(x_own, own)
     for swap in swaps:
         swap.wait()
     normalise(x_recv, other)
@@ -276,10 +283,10 @@
 
     lax.fori_loop(0, n_dq, dq_step, 0)
 
-    dkv_copy.wait()
-    kv_part[...] = lax.dot_general(a_chip[:, my_k], dkv_buf[...], NT, preferred_element_type=jnp.float32)
-    kv_copy = remote(kv_part.at[other, :], kv_recv, kv_send, kv_got)
-    kv_copy.start()
+    uk_copy.wait()
+    for index in range(my_heads // SWAP_BLOCK):
+        sel = slice(index * SWAP_BLOCK, (index + 1) * SWAP_BLOCK)
+        wuk_buf[index] = jnp.swapaxes(uk_buf[:, sel, :], 0, 1)
 
     for index in range(n_dq):
         cq_copy(index).wait()
@@ -299,7 +306,6 @@
     first = core == 0
     cos_t = jnp.concatenate([jnp.where(first, cos_own, cos_far), jnp.where(first, cos_far, cos_own)], axis=0)
     sin_t = jnp.concatenate([jnp.where(first, sin_own, sin_far), jnp.where(first, sin_far, sin_own)], axis=0)
-    uk_copy.wait()
 
     def head_cols(index):
         return pl.ds(pl.multiple_of(core * my_heads + index * SWAP_BLOCK, SWAP_BLOCK), SWAP_BLOCK)
@@ -323,7 +329,6 @@
         turned = []
         for sub in range(per_swap):
             uq_copy(index * per_swap + sub).wait()
-        wuk = jnp.swapaxes(uk_buf[:, pl.ds(pl.multiple_of(index * SWAP_BLOCK, SWAP_BLOCK), SWAP_BLOCK), :], 0, 1)
         for sub in range(per_swap):
             q_val = lax.dot_general(cq_chip[...], uq_buf[index * per_swap + sub], NT, preferred_element_type=jnp.float32)
             for head in range(HEAD_BLOCK):
@@ -332,7 +337,7 @@
                 low_half = q_val[:, base + nope_dim:base + nope_dim + half_dim]
                 high_half = q_val[:, base + nope_dim + half_dim:base + head_dim]
                 turned.append(jnp.concatenate([low_half * cos_t - high_half * sin_t, high_half * cos_t + low_half * sin_t], axis=1).astype(jnp.bfloat16))
-                absorbed.append(lax.dot_general(nope, wuk[sub * HEAD_BLOCK + head], NT, preferred_element_type=jnp.float32).astype(jnp.bfloat16))
+                absorbed.append(lax.dot_general(nope, wuk_buf[index, sub * HEAD_BLOCK + head], NT, preferred_element_type=jnp.float32).astype(jnp.bfloat16))
         abs_part[index] = jnp.swapaxes(jnp.stack(absorbed, axis=0), 0, 1)
         pe_part[index] = jnp.swapaxes(jnp.stack(turned, axis=0), 0, 1)
         for move in (abs_copy, pe_copy, abs_keep, pe_keep):
@@ -342,6 +347,10 @@
     n_swap = n_uq // per_swap
     lax.fori_loop(0, n_swap, uq_step, 0)
 
+    dkv_copy.wait()
+    kv_part[...] = lax.dot_general(a_chip[:, my_k], dkv_buf[...], NT, preferred_element_type=jnp.float32)
+    kv_copy = remote(kv_part.at[other, :], kv_recv, kv_send, kv_got)
+    kv_copy.start()
     kv_copy.wait()
     kv_val = kv_part[own, :] + kv_recv[...]
     latent = kv_val[:, :latent_dim]
@@ -377,13 +386,15 @@
             jax.ShapeDtypeStruct((rows, latent_dim), bf16),
             jax.ShapeDtypeStruct((rows, rope_dim), bf16),
         ],
-        in_specs=[vmem] * 6 + [anywhere] * 4,
+        in_specs=[anywhere] + [vmem] * 5 + [anywhere] * 4,
         out_specs=[anywhere, anywhere, vmem, vmem],
         scratch_shapes=[
             pltpu.VMEM((n_dq, d_model, DQ_W), bf16),
             pltpu.VMEM((kv_dim, d_model // 2), bf16),
             pltpu.VMEM((n_uq, HEAD_BLOCK * head_dim, q_rank), bf16),
             pltpu.VMEM((latent_dim, heads // 2, nope_dim), bf16),
+            pltpu.VMEM((n_swap, SWAP_BLOCK, latent_dim, nope_dim), bf16),
+            pltpu.VMEM((rows, d_model), bf16),
             pltpu.VMEM((rows, d_model), bf16),
             pltpu.VMEM((2, half_dim, rows), f32),
             pltpu.VMEM((2 * rows, d_model), bf16),
@@ -394,7 +405,7 @@
             pltpu.VMEM((n_swap, 2 * rows, SWAP_BLOCK, latent_dim), bf16),
             pltpu.VMEM((n_swap, 2 * rows, SWAP_BLOCK, rope_dim), bf16),
             pltpu.VMEM((rows, 1), f32),
-            dma((n_dq,)), dma(()), dma((n_uq,)), dma(()), dma((3,)), dma((3,)), dma((n_dq,)), dma((n_dq,)), dma(()), dma(()),
+            dma(()), dma((n_dq,)), dma(()), dma((n_uq,)), dma(()), dma((3,)), dma((3,)), dma((n_dq,)), dma((n_dq,)), dma(()), dma(()),
             dma((n_swap,)), dma((n_swap,)), dma((n_swap,)), dma((n_swap,)), dma((2, n_swap)),
         ],
         compiler_params=pltpu.CompilerParams(collective_id=1, has_side_effects=True, vmem_limit_bytes=66 * 1000 * 1000),
@@ -411,9 +422,9 @@
 
 
 def tail_kernel(o_ref, x_ref, gain_ref, wout_ref, wgate_ref, wup_ref, wdown_ref, out_ref,
-                slots, o_chip, x_chip, x_own, r_all, u_all, gate_buf, up_buf, act, sq_acc, pair_send, pair_recv, far_send, far_recv, own_sum,
+                slots, o_chip, x_chip, x_own, r_all, u_all, gate_buf, up_buf, act, sq_acc, pair_send, pair_recv, far_send, far_recv, own_sum, out_buf,
                 slot_sem, in_send, in_recv, loc_sem, rp_send, rp_recv, rx_send, rx_recv, rf_send, rf_recv,
-                pp_send, pp_recv, px_send, px_recv):
+                pp_send, pp_recv, px_send, px_recv, out_sem):
     rep, me, chip, core = _sides()
     part = chip * 2 + (1 - core)
     opp = (1 - chip) * 2 + core
@@ -667,14 +678,24 @@
     lax.fori_loop(0, n_half, settle, 0)
     own_rows = row_block(me)
 
+    def out_copy(index):
+        return pltpu.make_async_copy(out_buf.at[:, piece(index)], out_ref.at[:, piece(index)], out_sem.at[index])
+
     def finish(index, carry):
         far_copy(index).wait()
         pair_copy(index).wait_send()
         mlp = own_sum[index] + far_recv[index]
-        out_ref[:, piece(index)] = (r_all[index, own_rows, :].astype(jnp.float32) + mlp).astype(jnp.bfloat16)
+        out_buf[:, piece(index)] = (r_all[index, own_rows, :].astype(jnp.float32) + mlp).astype(jnp.bfloat16)
+        out_copy(index).start()
         return carry
 
     lax.fori_loop(0, n_all, finish, 0)
+
+    def flush(index, carry):
+        out_copy(index).wait()
+        return carry
+
+    lax.fori_loop(0, n_all, flush, 0)
 
 
 def tail(head_out, hidden, norm_mlp, w_out, w_gate, w_up, w_down):
@@ -692,7 +713,7 @@
         tail_kernel,
         out_shape=jax.ShapeDtypeStruct((rows, d_model), bf16),
         in_specs=[anywhere, anywhere, vmem, anywhere, anywhere, anywhere, anywhere],
-        out_specs=vmem,
+        out_specs=anywhere,
         scratch_shapes=[
             pltpu.VMEM((SLOTS, depth, OUT_W), bf16),
             pltpu.VMEM((2 * rows, attn_k), bf16),
@@ -709,9 +730,10 @@
             pltpu.VMEM((n_all, rows, PIECE), f32),
             pltpu.VMEM((n_all, rows, PIECE), f32),
             pltpu.VMEM((n_all, rows, PIECE), f32),
+            pltpu.VMEM((rows, d_model), bf16),
             dma((SLOTS,)), dma((2,)), dma((2,)), dma((3,)),
             dma((n_half,)), dma((n_half,)), dma((n_half,)), dma((n_half,)), dma((n_half,)), dma((n_half,)),
-            dma((n_all,)), dma((n_all,)), dma((n_all,)), dma((n_all,)),
+            dma((n_all,)), dma((n_all,)), dma((n_all,)), dma((n_all,)), dma((n_all,)),
         ],
         compiler_params=pltpu.CompilerParams(collective_id=0, has_side_effects=True, vmem_limit_bytes=66 * 1000 * 1000),
         name='tail',

time: 172 us -> 171 us (level); the launches traced: 172 us -> 173 us
  Pallas kernels: 169 us -> 171 us
    pallas_call x1, Pallas kernels: 115 us -> 118 us  [tail(): pl.pallas_call(tail_kernel, out_shape=jax.ShapeDtypeStruct((rows, d_model...]
where the time goes in v1:
time: 171 us; the launch traced here: 173 us
  Pallas kernels  171 us (100%)
  local copies, waits for them, and re-layouts  2.16 us (1%)
    pallas_call x1, Pallas kernels, tail(): pl.pallas_call(tail_kernel, out_shape=jax.ShapeDtypeStruct((rows, d_model...  118 us
    pallas_call x1, Pallas kernels, attend(): pl.pallas_call(functools.partial(attend_kernel, score_scale), out_shape=[...  26.8 us
    pallas_call x1, Pallas kernels, front(): pl.pallas_call(front_kernel, out_shape=[jax.ShapeDtypeStruct((rows, heads...  26.3 us

profile of v1, /device:TPU:0, one launch (start us, length us, event | category | flops | bytes accessed | tf_op | source)
XLA Modules:
  0.0 173.5 jit_solution(5276762753662738257)
XLA Ops:
  0.6 26.3 %front.1 = (bf16[64,64,512]{2,1,0:T(8,128)(2,1)}, bf16[64,64,64]{2,1,0:T(8,128)(2,1)}, bf16[64,512]{1,0:T(8,128)(2,1)}, bf16[64,64]{1,0:T(8,128)(2,1)}) custom-call(bf16[64,7168]{1,0:T(8,128)(2,1)} %x_ref.3, f32[1,7168]{1,0:T(1,128)} %bitcast.15, f32[12,128]{1,0:T(8,128)} %bitcast.19, f32[1,512]{1,0:T(1,128)} %bitcast.20, f32[32,64]{1,0:T(8,128)} %bitcast.17, ...), custom_call_target="tpu_custom_call" | custom-call | tf_op jit(solution)/shard_map/front/pallas_call | solution.py:381
  26.9 26.8 %attend.1 = (bf16[64,8192]{1,0:T(8,128)(2,1)}, bf16[64,512]{1,0:T(8,128)(2,1)}, bf16[64,64]{1,0:T(8,128)(2,1)}) custom-call(s32[64]{0:T(128)} %len_ref.1, bf16[64,64,512]{2,1,0:T(8,128)(2,1)} %get-tuple-element.10.abs_hbm, bf16[64,64,64]{2,1,0:T(8,128)(2,1)} %get-tuple-element.11.pe_hbm, bf16[64,512]{1,0:T(8,128)(2,1)} %get-tuple-element.12.new_ref, ...), custom_call_target="tpu_custom_call" | custom-call | tf_op jit(solution)/shard_map/attend/pallas_call | solution.py:160
  53.8 117.5 %tail.1 = bf16[64,7168]{1,0:T(8,128)(2,1)} custom-call(bf16[64,8192]{1,0:T(8,128)(2,1)} %get-tuple-element.14.o_ref, bf16[64,7168]{1,0:T(8,128)(2,1)} %x_ref.3, f32[1,7168]{1,0:T(1,128)} %bitcast.16, bf16[8192,7168]{1,0:T(8,128)(2,1)} %bitcast.10.wout_ref, bf16[7168,4608]{1,0:T(8,128)(2,1)} %wgate_ref.1, bf16[7168,4608]{1,0:T(8,128)(2,1)} %wup_ref.1, ...), custom_call_target="tpu_custom_call" | custom-call | tf_op jit(solution)/shard_map/tail/pallas_call | solution.py:712
  171.3 2.2 %copy.23 = bf16[64,7168]{1,0:T(8,128)(2,1)} copy(bf16[64,7168]{1,0:T(8,128)(2,1)} %tail.1) | data formatting | bytes 1835008

commit v2 on v1

--- a/solution.py
+++ b/solution.py
@@ -15,7 +15,7 @@
 OUT_W = 512
 PIECE = 256
 SLOTS = 4
-EARLY = 2
+EARLY = 1
 HEAD_BLOCK = 8
 SWAP_BLOCK = 16
 NT = (((1,), (1,)), ((), ()))

time: 171 us -> 171 us (level); the launches traced: 173 us -> 170 us
  Pallas kernels: 171 us -> 167 us
    pallas_call x1, Pallas kernels: 118 us -> 115 us  [tail(): pl.pallas_call(tail_kernel, out_shape=jax.ShapeDtypeStruct((rows, d_model...]
where the time goes in v2:
time: 171 us; the launch traced here: 170 us
  Pallas kernels  167 us (98%)
  local copies, waits for them, and re-layouts  2.16 us (1%)
    pallas_call x1, Pallas kernels, tail(): pl.pallas_call(tail_kernel, out_shape=jax.ShapeDtypeStruct((rows, d_model...  115 us
    pallas_call x1, Pallas kernels, attend(): pl.pallas_call(functools.partial(attend_kernel, score_scale), out_shape=[...  26.4 us
    pallas_call x1, Pallas kernels, front(): pl.pallas_call(front_kernel, out_shape=[jax.ShapeDtypeStruct((rows, heads...  26.3 us

profile of v2, /device:TPU:0, one launch (start us, length us, event | category | flops | bytes accessed | tf_op | source)
XLA Modules:
  0.0 170.2 jit_solution(15661684993619567950)
XLA Ops:
  0.6 26.3 %front.1 = (bf16[64,64,512]{2,1,0:T(8,128)(2,1)}, bf16[64,64,64]{2,1,0:T(8,128)(2,1)}, bf16[64,512]{1,0:T(8,128)(2,1)}, bf16[64,64]{1,0:T(8,128)(2,1)}) custom-call(bf16[64,7168]{1,0:T(8,128)(2,1)} %x_ref.3, f32[1,7168]{1,0:T(1,128)} %bitcast.15, f32[12,128]{1,0:T(8,128)} %bitcast.19, f32[1,512]{1,0:T(1,128)} %bitcast.20, f32[32,64]{1,0:T(8,128)} %bitcast.17, ...), custom_call_target="tpu_custom_call" | custom-call | tf_op jit(solution)/shard_map/front/pallas_call | solution.py:381
  26.9 26.4 %attend.1 = (bf16[64,8192]{1,0:T(8,128)(2,1)}, bf16[64,512]{1,0:T(8,128)(2,1)}, bf16[64,64]{1,0:T(8,128)(2,1)}) custom-call(s32[64]{0:T(128)} %len_ref.1, bf16[64,64,512]{2,1,0:T(8,128)(2,1)} %get-tuple-element.10.abs_hbm, bf16[64,64,64]{2,1,0:T(8,128)(2,1)} %get-tuple-element.11.pe_hbm, bf16[64,512]{1,0:T(8,128)(2,1)} %get-tuple-element.12.new_ref, ...), custom_call_target="tpu_custom_call" | custom-call | tf_op jit(solution)/shard_map/attend/pallas_call | solution.py:160
  53.3 114.7 %tail.1 = bf16[64,7168]{1,0:T(8,128)(2,1)} custom-call(bf16[64,8192]{1,0:T(8,128)(2,1)} %get-tuple-element.14.o_ref, bf16[64,7168]{1,0:T(8,128)(2,1)} %x_ref.3, f32[1,7168]{1,0:T(1,128)} %bitcast.16, bf16[8192,7168]{1,0:T(8,128)(2,1)} %bitcast.10.wout_ref, bf16[7168,4608]{1,0:T(8,128)(2,1)} %wgate_ref.1, bf16[7168,4608]{1,0:T(8,128)(2,1)} %wup_ref.1, ...), custom_call_target="tpu_custom_call" | custom-call | tf_op jit(solution)/shard_map/tail/pallas_call | solution.py:712
  168.0 2.2 %copy.23 = bf16[64,7168]{1,0:T(8,128)(2,1)} copy(bf16[64,7168]{1,0:T(8,128)(2,1)} %tail.1) | data formatting | bytes 1835008
